TPU v7x, 32 devices: a whole 2x2x4 slice. The times are simulated.
32 devices in a mesh: dp: 4 (over z), tensor: 8 (over y, x, core).
Axes of the slice: x: 2, y: 2, z: 4, core: 2. Of those that a mesh axis runs over, the one named last changes fastest.
Arguments:
- projected: bfloat16 [2, 4096, 4608], P(None, ('dp', 'tensor')), may hold values from -60 to 60
- out_grad: bfloat16 [2, 4096, 4608], P(None, ('dp', 'tensor')), may hold values from -20 to 20
- attention: bfloat16 [2, 4096, 4096], P(None, 'dp', 'tensor'), may hold values from -6 to 6
- w_out: bfloat16 [4096, 4608], P('tensor'), may hold values from -0.09375 to 0.09375
- gains: float32 [4608], replicated, may hold values from 0.5 to 1.5
- main_out: float32 [4096, 4608], P('tensor', 'dp'), may hold values from -6 to 6
- main_gains: float32 [4608], replicated, may hold values from -6 to 6
Outputs:
- attn_grad: bfloat16 [2, 4096, 4096], P(None, 'dp', 'tensor')
- new_main_out: float32 [4096, 4608], P('tensor', 'dp')
- new_main_gains: float32 [4608], replicated
All inputs are finite; a program needn't handle non-finite values.
Results may differ from a plain program's by a relative error of at most 0.0049.
Values may be sent and summed in bfloat16 or wider, within the bound.
A program may use at most 128 MiB of HBM per device.

v0:
```python
import functools
import math

import jax
import jax.numpy as jnp
from jax import lax
from jax.experimental import pallas as pl
from jax.experimental.pallas import tpu as pltpu
from jax.sharding import PartitionSpec as P

MESH = pl.DeviceIdType.MESH
LANES = 128
TILE = 16


def flip(index, step):
    return index + step * (1 - 2 * (lax.div(index, step) % 2))


def combine(index, steps):
    found = [index]
    for step in steps:
        found = found + [flip(each, step) for each in found]
    return found


def kernel(
    dims,
    factor,
    proj_hbm, grad_hbm, att_hbm, w_hbm, main_hbm, gains_ref,
    attn_hbm, sum_hbm, gain_hbm,
    own_in, held, w_buf, att_in, att_t, acc, part, arrived, out_sum, gain_acc, gain_mine, gain_got,
    in_sem, w_sem, att_sem, out_sem, main_sem,
    ag_send, ag_recv, pair_send, pair_recv, rs_send, rs_recv, gain_send, gain_recv,
):
    T, DP, D_true, micro, own, heads, wide, K = dims
    w = LANES
    R = micro * own
    L = (T // 2).bit_length() - 1
    C = T // 2
    t_me = lax.axis_index("tensor")
    d_me = lax.axis_index("dp")
    d_width = wide // DP
    t_pair = flip(t_me, 1)
    chip_steps = [2 << bit for bit in range(L)]
    cuts = [R * i // L // TILE * TILE for i in range(L)] + [R]

    blocks = 8
    height = R // blocks

    def load(block):
        slot = block % 2
        rows = pl.ds(block * height, height)
        return (
            pltpu.make_async_copy(proj_hbm.at[rows], own_in.at[slot, 0], in_sem.at[slot, 0]),
            pltpu.make_async_copy(grad_hbm.at[rows], own_in.at[slot, 1], in_sem.at[slot, 1]),
        )

    for block in range(2):
        for copy in load(block):
            copy.start()

    def att_load(t, slot):
        return [
            pltpu.make_async_copy(
                att_hbm.at[m, pl.ds(t * own, own)], att_in.at[slot, pl.ds(m * own, own)], att_sem.at[slot, m]
            )
            for m in range(micro)
        ]

    for t in range(2):
        for copy in att_load(t, t):
            copy.start()
    main_in = pltpu.make_async_copy(main_hbm, out_sum, main_sem)

    def w_load(k, d):
        return pltpu.make_async_copy(
            w_hbm.at[:, pl.ds(pl.multiple_of(d * d_width + k * w, w), w)],
            w_buf.at[k, :, pl.ds(d * w, w)],
            w_sem.at[k, d],
        )

    barrier = pltpu.get_barrier_semaphore()
    partners = [("tensor", t_pair)] + [("tensor", flip(t_me, step)) for step in chip_steps]
    dp_steps = [1 << bit for bit in range(DP.bit_length() - 1)]
    partners += [("dp", flip(d_me, step)) for step in dp_steps]
    for name, where in partners:
        pl.semaphore_signal(barrier, inc=1, device_id={name: where}, device_id_type=MESH)

    @pl.when(d_me > 0)
    def _():
        pl.semaphore_signal(barrier, inc=1, device_id={"dp": d_me - 1}, device_id_type=MESH)

    @pl.when(d_me < DP - 1)
    def _():
        pl.semaphore_signal(barrier, inc=1, device_id={"dp": d_me + 1}, device_id_type=MESH)

    gain_acc[...] = jnp.zeros_like(gain_acc)
    own_base = pl.multiple_of(t_me * R, R)
    for block in range(blocks):
        slot = block % 2
        for copy in load(block):
            copy.wait()

        def rows_step(i, carry, slot=slot, block=block):
            rows = pl.ds(pl.multiple_of(i * TILE, TILE), TILE)
            v = own_in[slot, 0, rows, :].astype(jnp.float32)
            g = own_in[slot, 1, rows, :].astype(jnp.float32)
            u = g * gains_ref[...].reshape(1, wide)
            r = lax.rsqrt(jnp.sum(v * v, axis=-1, keepdims=True) * (1.0 / D_true) + 1e-6)
            n = v * r
            m = jnp.sum(u * n, axis=-1, keepdims=True) * (1.0 / D_true)
            gn = g * n
            gain_acc[...] += gn[:8] + gn[8:]
            back = (r * (u - n * m)).astype(jnp.bfloat16)
            at = pl.ds(pl.multiple_of(own_base + block * height + i * TILE, TILE), TILE)
            for k in range(K):
                for d in range(DP):
                    c0 = d * d_width + k * w
                    held[k, at, d * w:(d + 1) * w] = back[:, c0:c0 + w]
            return carry

        lax.fori_loop(0, height // TILE, rows_step, 0)
        if block + 2 < blocks:
            for copy in load(block + 2):
                copy.start()
    gain_mine[0] = jnp.sum(gain_acc[...], axis=0, keepdims=True)

    waits = len(partners) + jnp.where(d_me > 0, 1, 0) + jnp.where(d_me < DP - 1, 1, 0)
    pl.semaphore_wait(barrier, waits)

    def block_of(k, t, p):
        if p is None:
            return held.at[k, pl.ds(pl.multiple_of(t * R, R), R)]
        return held.at[k, pl.ds(pl.multiple_of(t * R + cuts[p], TILE), cuts[p + 1] - cuts[p])]

    def stage_copies(k, s, receive):
        copies = []
        for p in range(L):
            bits = [chip_steps[(p + i) % L] for i in range(s + 1)]
            peer = flip(t_me, bits[s])
            first = peer if receive else t_me
            for j, src in enumerate(combine(first, bits[:s])):
                index = p * (C - 1) + (1 << s) - 1 + j
                ref = block_of(k, src, p)
                copies.append((p, index, src, pltpu.make_async_remote_copy(
                    src_ref=ref, dst_ref=ref, send_sem=ag_send.at[k, index], recv_sem=ag_recv.at[k, index],
                    device_id={"tensor": peer}, device_id_type=MESH)))
        return copies

    def pair_copy(k, index, src, p):
        ref = block_of(k, src, p)
        return pltpu.make_async_remote_copy(
            src_ref=ref, dst_ref=ref, send_sem=pair_send.at[k, index], recv_sem=pair_recv.at[k, index],
            device_id={"tensor": t_pair}, device_id_type=MESH)

    own_index = L * (C - 1)

    def advance(k, s):
        if s > 0:
            for p, index, src, copy in stage_copies(k, s - 1, True):
                copy.wait_recv()
                if s == L:
                    pair_copy(k, index, src, p).start()
        if s < L:
            for _, _, _, copy in stage_copies(k, s, False):
                copy.start()
            if s > 0:
                for p, index, src, _ in stage_copies(k, s - 1, True):
                    pair_copy(k, index, src, p).start()
            else:
                pair_copy(k, own_index, t_me, None).start()

    def all_received_from_pair(k):
        for s in range(L):
            for p, index, src, _ in stage_copies(k, s, True):
                pair_copy(k, index, flip(src, 1), p).wait_recv()
        pair_copy(k, own_index, t_pair, None).wait_recv()

    def all_sent(k):
        for s in range(L):
            for _, _, _, copy in stage_copies(k, s, False):
                copy.wait_send()
            for p, index, src, _ in stage_copies(k, s, True):
                pair_copy(k, index, src, p).wait_send()
        pair_copy(k, own_index, t_me, None).wait_send()

    def start_w(k, carry):
        for d in range(DP):
            w_load(k, d).start()
        return carry

    def rs_copy(k, d, to_left):
        if to_left:
            slot = jnp.where(d_me - 1 == d, DP, d)
            peer = d_me - 1
        else:
            slot, peer = d, d_me + 1
        return pltpu.make_async_remote_copy(
            src_ref=arrived.at[k, d], dst_ref=arrived.at[k, slot], send_sem=rs_send.at[k, d],
            recv_sem=rs_recv.at[k, slot], device_id={"dp": peer}, device_id_type=MESH)

    def rs_arrival(k, slot):
        return pltpu.make_async_remote_copy(
            src_ref=arrived.at[k, slot], dst_ref=arrived.at[k, slot], send_sem=rs_send.at[k, 0],
            recv_sem=rs_recv.at[k, slot], device_id={"dp": flip(d_me, 1)}, device_id_type=MESH)

    gain_steps = [("tensor", 1)] + [("tensor", s) for s in chip_steps] + [("dp", s) for s in dp_steps]
    S = len(gain_steps)

    def gain_copy(s):
        name, step = gain_steps[s]
        return pltpu.make_async_remote_copy(
            src_ref=gain_mine.at[s], dst_ref=gain_got.at[s], send_sem=gain_send.at[s], recv_sem=gain_recv.at[s],
            device_id={name: flip(t_me if name == "tensor" else d_me, step)}, device_id_type=MESH)

    def within(k):
        return jnp.logical_and(k >= 0, k < K)

    for q in range(min(L, K)):
        advance(q, 0)
    lax.fori_loop(0, K, start_w, 0)
    main_in.start()

    def turn(t, carry):
        slot = t % 2
        for copy in att_load(t, slot):
            copy.wait()
        att_t[:, pl.ds(pl.multiple_of(t * R, R), R)] = att_in[slot].astype(jnp.float32).T.astype(jnp.bfloat16)

        @pl.when(t + 2 < T)
        def _():
            for copy in att_load(t + 2, slot):
                copy.start()
        return carry

    lax.fori_loop(0, T // 2, turn, 0)
    advance(0, 1)
    lax.fori_loop(T // 2, T, turn, 0)
    main_in.wait()

    big = 2 * R
    tiles = T * R // big

    def step(i, carry):
        c = i - (L - 1)
        for s in range(L + 1):
            q = c + L - s

            @pl.when(jnp.logical_and(within(q), q >= (L if s == 0 else 1 if s == 1 else 0)))
            def _(q=q, s=s):
                advance(q, s)

        @pl.when(within(c))
        def _():
            all_received_from_pair(c)
            part[c % DP] = jnp.dot(att_t[...], held[c], preferred_element_type=jnp.float32)

        right = c - d_me
        left = c - (DP - 1 - d_me)
        final = jnp.minimum(left, right)

        def pass_on(k, d, to_left, has_arrival):
            piece = part[k % DP, :, d * w:(d + 1) * w]

            @pl.when(has_arrival)
            def _():
                rs_arrival(k, d).wait_recv()
                arrived[k, d] = (piece + arrived[k, d].astype(jnp.float32)).astype(jnp.bfloat16)

            @pl.when(jnp.logical_not(has_arrival))
            def _():
                arrived[k, d] = piece.astype(jnp.bfloat16)

            rs_copy(k, d, to_left).start()

        for d in reversed(range(1, DP)):
            @pl.when(jnp.logical_and(within(right), d_me < d))
            def _(d=d):
                pass_on(right, d, False, d_me > 0)
        for d in range(DP - 1):
            @pl.when(jnp.logical_and(within(left), d_me > d))
            def _(d=d):
                pass_on(left, d, True, d_me < DP - 1)

        @pl.when(within(c))
        def _():
            for d in range(DP):
                w_load(c, d).wait()

            def tile(n, carry):
                rows = pl.ds(pl.multiple_of(n * big, big), big)
                product = lax.dot_general(
                    held[c, rows, :], w_buf[c], (((1,), (1,)), ((), ())), preferred_element_type=jnp.float32)

                @pl.when(c == 0)
                def _():
                    acc[rows, :] = product

                @pl.when(c > 0)
                def _():
                    acc[rows, :] += product
                return carry

            lax.fori_loop(0, tiles, tile, 0)
            all_sent(c)

        @pl.when(c == K - 1)
        def _():
            def leave(t, carry):
                rows = pl.ds(pl.multiple_of(t * R, R), R)
                held[0, rows, :heads] = acc[rows, :].astype(jnp.bfloat16)
                for m in range(micro):
                    attn_copy(t, m).start()
                return carry
            lax.fori_loop(0, T, leave, 0)

        @pl.when(within(final))
        def _():
            mine = part[final % DP, :, pl.ds(pl.multiple_of(d_me * w, w), w)]
            at = pl.ds(pl.multiple_of(final * w, w), w)
            out_sum[:, at] += factor * mine

            @pl.when(d_me > 0)
            def _():
                rs_arrival(final, d_me).wait_recv()
                out_sum[:, at] += factor * arrived[final, d_me].astype(jnp.float32)

            @pl.when(d_me < DP - 1)
            def _():
                rs_arrival(final, DP).wait_recv()
                out_sum[:, at] += factor * arrived[final, DP].astype(jnp.float32)

        for s in range(S + 1):
            @pl.when(c == s)
            def _(s=s):
                if s > 0:
                    gain_copy(s - 1).wait()
                    gain_mine[s] = gain_mine[s - 1] + gain_got[s - 1]
                if s < S:
                    gain_copy(s).start()
        return carry

    def attn_copy(t, m):
        return pltpu.make_async_copy(
            held.at[0, pl.ds(pl.multiple_of(t * R + m * own, TILE), own), pl.ds(0, heads)],
            attn_hbm.at[m, pl.ds(pl.multiple_of(t * own, TILE), own)],
            out_sem.at[t, m],
        )

    total = max(K + DP - 1, S + 1)
    lax.fori_loop(0, total + L - 1, step, 0)

    sum_out = pltpu.make_async_copy(out_sum, sum_hbm, in_sem.at[0, 0])
    gain_out = pltpu.make_async_copy(gain_mine.at[S], gain_hbm, in_sem.at[0, 1])
    sum_out.start()
    gain_out.start()

    def drain(k, carry):
        for d in range(DP):
            @pl.when(d != d_me)
            def _(d=d):
                pltpu.make_async_remote_copy(
                    src_ref=arrived.at[k, d], dst_ref=arrived.at[k, d], send_sem=rs_send.at[k, d],
                    recv_sem=rs_recv.at[k, d], device_id={"dp": flip(d_me, 1)}, device_id_type=MESH).wait_send()
        return carry

    lax.fori_loop(0, K, drain, 0)

    def attn_wait(t, carry):
        for m in range(micro):
            attn_copy(t, m).wait()
        return carry

    lax.fori_loop(0, T, attn_wait, 0)
    sum_out.wait()
    gain_out.wait()


def padded(values, parts, axis):
    size = values.shape[axis] // parts
    extra = -size % LANES
    if extra == 0:
        return values
    shape = values.shape
    split = values.reshape(shape[:axis] + (parts, size) + shape[axis + 1:])
    pads = [(0, 0)] * split.ndim
    pads[axis + 1] = (0, extra)
    return jnp.pad(split, pads).reshape(shape[:axis] + (parts * (size + extra),) + shape[axis + 1:])


def unpadded(values, parts, size, axis):
    have = values.shape[axis] // parts
    if have == size:
        return values
    shape = values.shape
    split = values.reshape(shape[:axis] + (parts, have) + shape[axis + 1:])
    split = lax.slice_in_dim(split, 0, size, axis=axis + 1)
    return split.reshape(shape[:axis] + (parts * size,) + shape[axis + 1:])


def per_device(projected, out_grad, attention, w_out, gains, main_out, main_gains):
    T, DP = lax.axis_size("tensor"), lax.axis_size("dp")
    micro, own, D = projected.shape
    heads = w_out.shape[0]
    piece = D // DP
    factor = 1.0 / math.sqrt(micro * own * DP * T)
    R = micro * own
    proj = padded(projected.reshape(R, D), DP, 1)
    grad = padded(out_grad.reshape(R, D), DP, 1)
    weight = padded(w_out, DP, 1)
    gain_row = padded(gains, DP, 0)
    main = padded(main_out, 1, 1)
    wide = proj.shape[1]
    K = wide // DP // LANES
    C = T // 2
    L = C.bit_length() - 1
    S = 1 + L + DP.bit_length() - 1
    chunk = DP * LANES
    dims = (T, DP, D, micro, own, heads, wide, K)
    count = L * (C - 1)
    DMA = pltpu.SemaphoreType.DMA
    anywhere = pl.BlockSpec(memory_space=pl.ANY)
    attn_grad, total, gain_total = pl.pallas_call(
        functools.partial(kernel, dims, factor),
        out_shape=(
            jax.ShapeDtypeStruct((micro, own * T, heads), jnp.bfloat16),
            jax.ShapeDtypeStruct((heads, wide // DP), jnp.float32),
            jax.ShapeDtypeStruct((1, wide), jnp.float32),
        ),
        in_specs=[anywhere] * 5 + [pl.BlockSpec(memory_space=pltpu.VMEM)],
        out_specs=(anywhere,) * 3,
        scratch_shapes=[
            pltpu.VMEM((2, 2, R // 8, wide), jnp.bfloat16),
            pltpu.VMEM((K, T * R, chunk), jnp.bfloat16),
            pltpu.VMEM((K, heads, chunk), jnp.bfloat16),
            pltpu.VMEM((2, R, heads), jnp.bfloat16),
            pltpu.VMEM((heads, T * R), jnp.bfloat16),
            pltpu.VMEM((T * R, heads), jnp.float32),
            pltpu.VMEM((DP, heads, chunk), jnp.float32),
            pltpu.VMEM((K, DP + 1, heads, LANES), jnp.bfloat16),
            pltpu.VMEM((heads, wide // DP), jnp.float32),
            pltpu.VMEM((8, wide), jnp.float32),
            pltpu.VMEM((S + 1, 1, wide), jnp.float32),
            pltpu.VMEM((S, 1, wide), jnp.float32),
            DMA((2, 2)), DMA((K, DP)), DMA((2, micro)), DMA((T, micro)), DMA,
            DMA((K, count)), DMA((K, count)), DMA((K, count + 1)), DMA((K, count + 1)),
            DMA((K, DP)), DMA((K, DP + 1)), DMA((S,)), DMA((S,)),
        ],
        compiler_params=pltpu.CompilerParams(
            collective_id=0, has_side_effects=True, vmem_limit_bytes=67043328
        ),
    )(proj, grad, attention, weight, main, gain_row)
    total = unpadded(total, 1, piece, 1)
    gain_total = unpadded(gain_total, DP, piece, 1).reshape(D)
    return (attn_grad, total, main_gains + factor * gain_total)


def solution(mesh):
    placed = (
        P(None, ("dp", "tensor"), None),
        P(None, ("dp", "tensor"), None),
        P(None, "dp", "tensor"),
        P("tensor", None),
        P(),
        P("tensor", "dp"),
        P(),
    )
    return jax.shard_map(
        per_device,
        mesh=mesh,
        in_specs=placed,
        out_specs=(P(None, "dp", "tensor"), P("tensor", "dp"), P()),
        check_vma=False,
    )
```

profile of v0, /device:TPU:0, one launch (start us, length us, event | category | flops | bytes accessed | tf_op | source)
XLA Modules:
  0.0 121.5 jit_solution(10125256662240202161)
XLA Ops:
  0.6 114.2 %shard_map.94 = (bf16[2,1024,512]{2,1,0:T(8,128)(2,1)}, f32[512,1152]{1,0:T(8,128)}, f32[1,4608]{1,0:T(1,128)}) custom-call(bf16[256,4608]{1,0:T(8,128)(2,1)} %bitcast.2, bf16[256,4608]{1,0:T(8,128)(2,1)} %bitcast.3, bf16[2,1024,512]{2,1,0:T(8,128)(2,1)} %att_hbm.1, bf16[512,4608]{1,0:T(8,128)(2,1)} %w_hbm.1, f32[512,1152]{1,0:T(8,128)} %main_hbm.1, ...), custom_call_target="tpu_custom_call" | custom-call | tf_op jit(solution)/shard_map/pallas_call | solution.py:424
  114.8 0.0 copy-start
  114.8 0.9 multiply_reduce_fusion
  115.7 1.3 %add.3 = f32[4608]{0:T(1024)} add(f32[4608]{0:T(1024)} %param.13, f32[4608]{0:T(1024)S(1)} %multiply_reduce_fusion) | non-fusion elementwise | flops 4608 | bytes 55296 | tf_op jit(solution)/shard_map/add | solution.py:456
  117.1 3.0 %copy.12 = bf16[2,1024,512]{2,1,0:T(8,128)(2,1)} copy(bf16[2,1024,512]{2,1,0:T(8,128)(2,1)} %get-tuple-element.12) | data formatting | bytes 4194304
  120.1 0.0 copy-done
  120.1 1.4 %copy.13 = f32[512,1152]{1,0:T(8,128)} copy(f32[512,1152]{1,0:T(8,128)S(1)} %copy-done) | data formatting | bytes 4718592
Async XLA Ops:
  114.8 5.3 %copy-start = (f32[512,1152]{1,0:T(8,128)S(1)}, f32[512,1152]{1,0:T(8,128)}, u32[]{:S(2)}) copy-start(f32[512,1152]{1,0:T(8,128)} %get-tuple-element.13) | copy-start | bytes 7077892
where the time goes:
time: 122 us
  Pallas kernels  114 us (93%)
  local copies, waits for them, and re-layouts  4.45 us (4%)
  other arithmetic  2.26 us (2%)
    pallas_call x1, Pallas kernels, per_device(): pl.pallas_call(functools.partial(kernel, dims, factor), out_shape=(jax.Sh...  114 us
    unnamed x4, local copies, waits for them, and re-layouts  4.45 us

commit v1 on v0

v1 whole, which is shorter than its diff:
```python
import functools
import math

import jax
import jax.numpy as jnp
from jax import lax
from jax.experimental import pallas as pl
from jax.experimental.pallas import tpu as pltpu
from jax.sharding import PartitionSpec as P

MESH = pl.DeviceIdType.MESH
LANES = 128
TILE = 16
VMEM_BYTES = 67043328


def flip(index, step):
    return index + step * (1 - 2 * (lax.div(index, step) % 2))


HOP = 3
LEAD = 3
GAP = 4


def kernel(
    dims,
    factor,
    proj_hbm, grad_hbm, att_hbm, w_hbm, main_hbm, gains_ref, main_gains_ref,
    attn_out, out_sum, gain_out,
    own_in, held, w_buf, att_in, att_t, acc, part, arrived,
    gains_row, scale, shift, gain_mine, gain_got,
    in_sem, w_sem, att_sem, main_sem,
    ag_send, ag_recv, pair_send, pair_recv, rs_send, rs_recv, gain_send, gain_recv,
):
    T, DP, D_true, micro, own, heads, wide, K, slots, ring, P, W = dims
    w = LANES
    R = micro * own
    L = (T // 2).bit_length() - 1
    C = T // 2
    O = DP - 1
    t_me = lax.axis_index("tensor")
    d_me = lax.axis_index("dp")
    c_me, chip_me = t_me % 2, lax.div(t_me, 2)
    d_width = wide // DP
    t_pair = flip(t_me, 1)
    chip_steps = [2 << bit for bit in range(L)]
    height = R // P
    span = C * R
    end = (K + O) * DP

    blocks = 8
    group = R // blocks

    def load(block):
        rows = pl.ds(block * group, group)
        return (
            pltpu.make_async_copy(proj_hbm.at[rows], own_in.at[0, rows], in_sem.at[block, 0]),
            pltpu.make_async_copy(grad_hbm.at[rows], own_in.at[1, rows], in_sem.at[block, 1]),
        )

    for block in range(blocks):
        for copy in load(block):
            copy.start()

    def att_load(t, slot):
        return [
            pltpu.make_async_copy(
                att_hbm.at[m, pl.ds(t * own, own)], att_in.at[slot, pl.ds(m * own, own)], att_sem.at[slot, m]
            )
            for m in range(micro)
        ]

    for t in range(slots):
        for copy in att_load(t, t):
            copy.start()
    main_in = pltpu.make_async_copy(main_hbm, out_sum, main_sem)

    def w_load(k, d):
        return pltpu.make_async_copy(
            w_hbm.at[:, pl.ds(pl.multiple_of(d * d_width + k * w, w), w)],
            w_buf.at[k, :, pl.ds(d * w, w)],
            w_sem,
        )

    barrier = pltpu.get_barrier_semaphore()
    partners = [("tensor", t_pair)] + [("tensor", flip(t_me, step)) for step in chip_steps]
    dp_steps = [1 << bit for bit in range(DP.bit_length() - 1)]
    partners += [("dp", flip(d_me, step)) for step in dp_steps]
    for name, where in partners:
        pl.semaphore_signal(barrier, inc=1, device_id={name: where}, device_id_type=MESH)

    @pl.when(d_me > 0)
    def _():
        pl.semaphore_signal(barrier, inc=1, device_id={"dp": d_me - 1}, device_id_type=MESH)

    @pl.when(d_me < DP - 1)
    def _():
        pl.semaphore_signal(barrier, inc=1, device_id={"dp": d_me + 1}, device_id_type=MESH)

    def place(n):
        s, j = lax.div(n, DP), lax.rem(n, DP)
        right = DP - 1 - d_me
        down = jnp.where(j < right, DP - 1 - j, j - right)
        up = jnp.where(j < d_me, j, DP - 1 - (j - d_me))
        d = jnp.where(j == DP - 1, d_me, jnp.where(2 * d_me < DP, down, up))
        lag = jnp.where(d > d_me, DP - 1 - d, jnp.where(d < d_me, d, O))
        k = s - lag
        good = jnp.logical_and(n >= 0, jnp.logical_and(k >= 0, k < K))
        return k, d, good

    def following(n):
        n = n + 1
        for _ in range(DP - 1):
            n = jnp.where(jnp.logical_or(place(n)[2], n >= end), n, n + 1)
        return n

    def turned(chip, p):
        return lax.div(chip, 1 << p) + (chip % (1 << p)) * (1 << (L - p))

    def home(parity, p, index):
        return pl.multiple_of(parity * span + (p * C + index) * height, LANES)

    gains_row[...] = gains_ref[...].reshape(1, wide)
    for block in range(blocks):
        for copy in load(block):
            copy.wait()

        def rows_step(i, carry, block=block):
            rows = pl.ds(pl.multiple_of(block * group + i * TILE, TILE), TILE)
            square = jnp.zeros((TILE, w), jnp.float32)
            cross = jnp.zeros((TILE, w), jnp.float32)
            for c0 in range(0, wide, w):
                v = own_in[0, rows, c0:c0 + w].astype(jnp.float32)
                g = own_in[1, rows, c0:c0 + w].astype(jnp.float32)
                square += v * v
                cross += (g * gains_row[:, c0:c0 + w]) * v
            r = lax.rsqrt(jnp.sum(square, axis=-1, keepdims=True) * (1.0 / D_true) + 1e-6)
            m = r * jnp.sum(cross, axis=-1, keepdims=True) * (1.0 / D_true)
            scale[rows, :] = jnp.broadcast_to(r, (TILE, w))
            shift[rows, :] = jnp.broadcast_to(r * m, (TILE, w))
            return carry

        lax.fori_loop(0, group // TILE, rows_step, 0)

    base = [home(c_me, p, turned(chip_me, p)) for p in range(P)]
    strip = 64

    def finish(n):
        k, d, good = place(n)

        @pl.when(good)
        def _():
            columns = pl.ds(pl.multiple_of(d * d_width + k * w, w), w)
            gain = gains_row[:, columns]
            total = jnp.zeros((8, w), jnp.float32)
            for i in range(0, R, strip):
                rows = pl.ds(i, strip)
                v = own_in[0, rows, columns].astype(jnp.float32)
                g = own_in[1, rows, columns].astype(jnp.float32)
                r = scale[rows, :]
                back = r * (g * gain - v * shift[rows, :])
                at = pl.ds(pl.multiple_of(base[i // height] + i % height, TILE), strip)
                held[k, d, at, :] = back.astype(jnp.bfloat16)
                gn = g * (v * r)
                for b in range(0, strip, 8):
                    total += gn[b:b + 8]
            gain_mine[0, :, columns] = jnp.sum(total, axis=0, keepdims=True)

    def grown(p, s, theirs):
        index = turned(chip_me, p)
        if theirs:
            index = flip(index, 1 << s)
        return pl.ds(home(c_me, p, lax.div(index, 1 << s) * (1 << s)), height << s)

    sent = [[grown(p, s, False) for p in range(P)] for s in range(L)]
    got = [[grown(p, s, True) for p in range(P)] for s in range(L)]

    def stage_copies(k, d, c, s, receive):
        copies = []
        for p in range(P):
            ref = held.at[k, d, (got if receive else sent)[s][p]]
            copies.append(pltpu.make_async_remote_copy(
                src_ref=ref, dst_ref=ref, send_sem=ag_send, recv_sem=ag_recv.at[c % W, s, p],
                device_id={"tensor": flip(t_me, chip_steps[(p + s) % L])}, device_id_type=MESH))
        return copies

    def half(parity):
        return pl.ds(pl.multiple_of(parity * span, span), span)

    def pair_copy(k, d, c, parity):
        ref = held.at[k, d, half(parity)]
        return pltpu.make_async_remote_copy(
            src_ref=ref, dst_ref=ref, send_sem=pair_send, recv_sem=pair_recv.at[c % W],
            device_id={"tensor": t_pair}, device_id_type=MESH)

    def advance(n, c, s, when=True):
        k, d, good = place(n)

        @pl.when(jnp.logical_and(good, when))
        def _():
            if s > 0:
                for copy in stage_copies(k, d, c, s - 1, True):
                    copy.wait_recv()
            if s < L:
                for copy in stage_copies(k, d, c, s, False):
                    copy.start()
            else:
                pair_copy(k, d, c, c_me).start()

    def start_w(k, carry):
        for d in range(DP):
            w_load(k, d).start()
        return carry

    def rs_copy(k, d, to_left):
        if to_left:
            slot = jnp.where(d_me - 1 == d, DP, d)
            peer = d_me - 1
        else:
            slot, peer = d, d_me + 1
        return pltpu.make_async_remote_copy(
            src_ref=arrived.at[k, d], dst_ref=arrived.at[k, slot], send_sem=rs_send,
            recv_sem=rs_recv.at[k, slot], device_id={"dp": peer}, device_id_type=MESH)

    def rs_arrival(k, slot):
        return pltpu.make_async_remote_copy(
            src_ref=arrived.at[k, slot], dst_ref=arrived.at[k, slot], send_sem=rs_send,
            recv_sem=rs_recv.at[k, slot], device_id={"dp": flip(d_me, 1)}, device_id_type=MESH)

    gain_steps = [("tensor", 1)] + [("tensor", s) for s in chip_steps] + [("dp", s) for s in dp_steps]
    S = len(gain_steps)

    def gain_copy(s):
        name, step = gain_steps[s]
        return pltpu.make_async_remote_copy(
            src_ref=gain_mine.at[s], dst_ref=gain_got.at[s], send_sem=gain_send.at[s], recv_sem=gain_recv.at[s],
            device_id={name: flip(t_me if name == "tensor" else d_me, step)}, device_id_type=MESH)

    look = [LEAD + GAP * (L - 1 - s) for s in range(L)]
    ahead = [jnp.int32(0)] * L

    def turn(t, carry):
        slot = t % slots
        for copy in att_load(t, slot):
            copy.wait()
        flat = att_in[slot].astype(jnp.float32).T.astype(jnp.bfloat16)
        for p in range(P):
            at = pl.ds(home(t % 2, p, turned(lax.div(t, 2), p)), height)
            att_t[:, at] = flat[:, p * height:(p + 1) * height]

        @pl.when(t + slots < T)
        def _():
            for copy in att_load(t + slots, slot):
                copy.start()
        return carry

    finish(ahead[0])
    waits = len(partners) + jnp.where(d_me > 0, 1, 0) + jnp.where(d_me < DP - 1, 1, 0)
    pl.semaphore_wait(barrier, waits)
    for i in range(look[0]):
        if i == look[0] - look[1] if L > 1 else i == look[0] - 1:
            lax.fori_loop(0, K, start_w, 0)
            main_in.start()
            lax.fori_loop(0, T, turn, 0)
        for s in reversed(range(L)):
            if i - look[0] + look[s] >= 0:
                if s == 0 and i > 0:
                    finish(ahead[0])
                advance(ahead[s], i - look[0] + look[s], s)
                ahead[s] = following(ahead[s])
    finish(ahead[0])
    main_in.wait()

    big = T * R // DP
    gain_from = (K * DP - look[0] + 1) // 2 + DP * (DP - 1) // 2 + 1

    def pass_on(n, to_left):
        k, d, good = place(n)
        mine = (d < d_me) if to_left else (d > d_me)
        has_arrival = (d_me < DP - 1) if to_left else (d_me > 0)

        @pl.when(jnp.logical_and(good, mine))
        def _():
            @pl.when(has_arrival)
            def _():
                rs_arrival(k, d).wait_recv()
                arrived[k, d] = (part[k % ring, d] + arrived[k, d].astype(jnp.float32)).astype(jnp.bfloat16)

            @pl.when(jnp.logical_not(has_arrival))
            def _():
                arrived[k, d] = part[k % ring, d].astype(jnp.bfloat16)

            rs_copy(k, d, to_left).start()

    def step(n, carry):
        done, late, todo, ahead = carry[0], carry[1], carry[2], list(carry[3:])
        k, d, good = place(n)
        advance(n, done, L)
        for s in reversed(range(L)):
            advance(ahead[s], done + look[s], s, good)
            ahead[s] = jnp.where(good, following(ahead[s]), ahead[s])

        first = jnp.logical_and(good, done == 0)
        ripe = jnp.logical_or(first, jnp.logical_and(late >= 0, jnp.logical_or(good, n - late >= 2)))
        chosen = jnp.where(ripe, jnp.where(first, n, late), -1)
        count = jnp.where(first, done, done - 1)

        @pl.when(ripe)
        def _():
            k, d, _ = place(chosen)
            pair_copy(k, d, count, 1 - c_me).wait_recv()
            part[k % ring, d] = jnp.dot(att_t[...], held[k, d], preferred_element_type=jnp.float32)

        pass_on(jnp.where(d_me == 0, chosen, n - HOP * d_me), False)
        pass_on(jnp.where(d_me == DP - 1, chosen, n - HOP * (DP - 1 - d_me)), True)

        for _ in range(2):
            @pl.when(good)
            def _(todo=todo):
                finish(todo)
            todo = jnp.where(good, following(todo), todo)
        c = lax.div(n - 2, DP) - O - 1
        j = lax.rem(n - 2, DP)

        @pl.when(jnp.logical_and(c >= 0, c < K))
        def _():
            @pl.when(j == 0)
            def _():
                @pl.when(c == 0)
                def _():
                    pltpu.make_async_copy(w_buf, w_buf, w_sem).wait()
            rows = pl.ds(pl.multiple_of(j * big, big), big)
            lhs = jnp.concatenate([held[c, e, rows, :] for e in range(DP)], axis=-1)
            value = lax.dot_general(
                lhs, w_buf[c], (((1,), (1,)), ((), ())), preferred_element_type=jnp.float32)

            @pl.when(c == 0)
            def _():
                acc[rows, :] = value

            @pl.when(jnp.logical_and(c > 0, c < K - 1))
            def _():
                acc[rows, :] += value

            @pl.when(c == K - 1)
            def _():
                last = (acc[rows, :] + value).astype(jnp.bfloat16)
                units, each = C * height // LANES, height // LANES
                for i in range(big // LANES):
                    at = j * (big // LANES) + i
                    parity, rest = lax.div(at, P * units), lax.rem(at, P * units)
                    p, rest = lax.div(rest, units), lax.rem(rest, units)
                    index, extra = lax.div(rest, each), lax.rem(rest, each)
                    chip = turned(index, 0)
                    for q in range(1, P):
                        chip = jnp.where(p == q, turned(index, L - q), chip)
                    row = p * height + extra * LANES
                    m, row = lax.div(row, own), lax.rem(row, own)
                    place_in = pl.ds(pl.multiple_of((chip * 2 + parity) * own + row, LANES), LANES)
                    attn_out[m, place_in, :] = last[i * LANES:(i + 1) * LANES]

        @pl.when(jnp.logical_and(jnp.logical_and(c >= 0, c < K), j == DP - 1))
        def _():
            at = pl.ds(pl.multiple_of(c * w, w), w)
            total = part[c % ring, d_me]
            out_sum[:, at] += factor * total

            @pl.when(d_me > 0)
            def _():
                rs_arrival(c, d_me).wait_recv()
                out_sum[:, at] += factor * arrived[c, d_me].astype(jnp.float32)

            @pl.when(d_me < DP - 1)
            def _():
                rs_arrival(c, DP).wait_recv()
                out_sum[:, at] += factor * arrived[c, DP].astype(jnp.float32)

        for s in range(S + 1):
            @pl.when(n == gain_from + 2 * s)
            def _(s=s):
                if s > 0:
                    gain_copy(s - 1).wait()
                    gain_mine[s] = gain_mine[s - 1] + gain_got[s - 1]
                if s < S:
                    gain_copy(s).start()
                else:
                    gain_out[...] = main_gains_ref[...] + factor * gain_mine[s].reshape(wide)

        late = jnp.where(
            jnp.logical_and(good, jnp.logical_not(first)), n, jnp.where(ripe, -1, late))
        return (done + jnp.where(good, 1, 0), late, todo, *ahead)

    total = max(end + DP + 2, gain_from + 2 * S + 1)
    lax.fori_loop(0, total, step, (jnp.int32(0), jnp.int32(-1), following(ahead[0]), *ahead))

    def sent_all(ref, sem):
        pltpu.make_async_remote_copy(
            src_ref=ref, dst_ref=ref, send_sem=sem, recv_sem=sem,
            device_id={"tensor": t_pair}, device_id_type=MESH).wait_send()

    sent_all(held.at[:, :, pl.ds(0, (C - 1) * R)], ag_send)
    sent_all(held.at[:, :, pl.ds(0, span)], pair_send)
    sent_all(arrived.at[:, pl.ds(0, DP - 1)], rs_send)


def emit(attn, total, gain, attn_hbm, total_hbm, gain_hbm, sem):
    copies = [
        pltpu.make_async_copy(attn, attn_hbm, sem.at[0]),
        pltpu.make_async_copy(total, total_hbm, sem.at[1]),
        pltpu.make_async_copy(gain, gain_hbm, sem.at[2]),
    ]
    for copy in copies:
        copy.start()
    for copy in copies:
        copy.wait()


def padded(values, parts, axis):
    size = values.shape[axis] // parts
    extra = -size % LANES
    if extra == 0:
        return values
    shape = values.shape
    split = values.reshape(shape[:axis] + (parts, size) + shape[axis + 1:])
    pads = [(0, 0)] * split.ndim
    pads[axis + 1] = (0, extra)
    return jnp.pad(split, pads).reshape(shape[:axis] + (parts * (size + extra),) + shape[axis + 1:])


def unpadded(values, parts, size, axis):
    have = values.shape[axis] // parts
    if have == size:
        return values
    shape = values.shape
    split = values.reshape(shape[:axis] + (parts, have) + shape[axis + 1:])
    split = lax.slice_in_dim(split, 0, size, axis=axis + 1)
    return split.reshape(shape[:axis] + (parts * size,) + shape[axis + 1:])


def per_device(projected, out_grad, attention, w_out, gains, main_out, main_gains):
    T, DP = lax.axis_size("tensor"), lax.axis_size("dp")
    micro, own, D = projected.shape
    heads = w_out.shape[0]
    piece = D // DP
    factor = 1.0 / math.sqrt(micro * own * DP * T)
    R = micro * own
    proj = padded(projected.reshape(R, D), DP, 1)
    grad = padded(out_grad.reshape(R, D), DP, 1)
    weight = padded(w_out, DP, 1)
    gain_row = padded(gains, DP, 0)
    main_gain_row = padded(main_gains, DP, 0)
    main = padded(main_out, 1, 1)
    wide = proj.shape[1]
    K = wide // DP // LANES
    C = T // 2
    L = C.bit_length() - 1
    S = 1 + L + DP.bit_length() - 1
    slots = 4
    ring = HOP * (DP - 1) // DP + 1
    P = min(L, R // LANES)
    P = P if R // LANES % P == 0 else 1
    W = 1 << (LEAD + GAP * (L - 1)).bit_length()
    dims = (T, DP, D, micro, own, heads, wide, K, slots, ring, P, W)
    DMA = pltpu.SemaphoreType.DMA
    hbm = pl.BlockSpec(memory_space=pltpu.HBM)
    vmem = pl.BlockSpec(memory_space=pltpu.VMEM)
    shapes = (
        ((micro, own * T, heads), jnp.bfloat16),
        ((heads, wide // DP), jnp.float32),
        ((wide,), jnp.float32),
    )
    kept = sum(math.prod(shape) * jnp.dtype(dtype).itemsize for shape, dtype in shapes) + (64 << 10)
    results = pl.pallas_call(
        functools.partial(kernel, dims, factor),
        out_shape=tuple(pltpu.VMEM(shape, dtype) for shape, dtype in shapes),
        in_specs=[hbm] * 5 + [vmem] * 2,
        out_specs=(vmem,) * 3,
        scratch_shapes=[
            pltpu.VMEM((2, R, wide), jnp.bfloat16),
            pltpu.VMEM((K, DP, T * R, LANES), jnp.bfloat16),
            pltpu.VMEM((K, heads, DP * LANES), jnp.bfloat16),
            pltpu.VMEM((slots, R, heads), jnp.bfloat16),
            pltpu.VMEM((heads, T * R), jnp.bfloat16),
            pltpu.VMEM((T * R, heads), jnp.float32),
            pltpu.VMEM((ring, DP, heads, LANES), jnp.float32),
            pltpu.VMEM((K, DP + 1, heads, LANES), jnp.bfloat16),
            pltpu.VMEM((1, wide), jnp.float32),
            pltpu.VMEM((R, LANES), jnp.float32),
            pltpu.VMEM((R, LANES), jnp.float32),
            pltpu.VMEM((S + 1, 1, wide), jnp.float32),
            pltpu.VMEM((S, 1, wide), jnp.float32),
            DMA((8, 2)), DMA, DMA((slots, micro)), DMA,
            DMA, DMA((W, L, P)), DMA, DMA((W,)), DMA, DMA((K, DP + 1)), DMA((S,)), DMA((S,)),
        ],
        compiler_params=pltpu.CompilerParams(
            collective_id=0, has_side_effects=True, vmem_limit_bytes=VMEM_BYTES - kept
        ),
    )(proj, grad, attention, weight, main, gain_row, main_gain_row)
    attn_grad, total, gain_total = pl.pallas_call(
        emit,
        out_shape=tuple(jax.ShapeDtypeStruct(shape, dtype) for shape, dtype in shapes),
        in_specs=[vmem] * 3,
        out_specs=(hbm,) * 3,
        scratch_shapes=[DMA((3,))],
        compiler_params=pltpu.CompilerParams(vmem_limit_bytes=1 << 20),
    )(*results)
    total = unpadded(total, 1, piece, 1)
    gain_total = unpadded(gain_total, DP, piece, 0).reshape(D)
    return (attn_grad, total, gain_total)


def solution(mesh):
    placed = (
        P(None, ("dp", "tensor"), None),
        P(None, ("dp", "tensor"), None),
        P(None, "dp", "tensor"),
        P("tensor", None),
        P(),
        P("tensor", "dp"),
        P(),
    )
    return jax.shard_map(
        per_device,
        mesh=mesh,
        in_specs=placed,
        out_specs=(P(None, "dp", "tensor"), P("tensor", "dp"), P()),
        check_vma=False,
    )
```

time: 122 us -> 110 us (0.902)
  Pallas kernels: 114 us -> 108 us
  local copies, waits for them, and re-layouts: 4.45 us -> 0 us
  other arithmetic: 2.26 us -> 0 us
    pallas_call x1 -> x2, Pallas kernels: 114 us -> 108 us  [the longest x1 106 us: per_device(): pl.pallas_call(functools.partial(kernel, dims, factor), out_shape=tuple((...]
    unnamed x4 -> x0, local copies, waits for them, and re-layouts: 4.45 us -> none
    add x1 -> x0, other arithmetic: 1.34 us -> none  [per_device(): return (attn_grad, total, main_gains + factor * gain_total)]
where the time goes in v1:
time: 110 us; the launch traced here: 108 us
  Pallas kernels  108 us (98%)
    pallas_call x1, Pallas kernels, per_device(): pl.pallas_call(functools.partial(kernel, dims, factor), out_shape=tuple((...  106 us

profile of v1, /device:TPU:0, one launch (start us, length us, event | category | flops | bytes accessed | tf_op | source)
XLA Modules:
  0.0 108.4 jit_solution(13897612970446457281)
XLA Ops:
  0.6 105.6 %shard_map.94 = (bf16[2,1024,512]{2,1,0:T(8,128)(2,1)S(1)}, f32[512,1152]{1,0:T(8,128)S(1)}, f32[4608]{0:T(1024)S(1)}) custom-call(bf16[256,4608]{1,0:T(8,128)(2,1)} %bitcast.2, bf16[256,4608]{1,0:T(8,128)(2,1)} %bitcast.3, bf16[2,1024,512]{2,1,0:T(8,128)(2,1)} %att_hbm.1, bf16[512,4608]{1,0:T(8,128)(2,1)} %w_hbm.1, f32[512,1152]{1,0:T(8,128)} %main_hbm.1, ...), custom_call_target="tpu_custom_call" | custom-call | tf_op jit(solution)/shard_map/pallas_call | solution.py:474
  106.3 2.1 %shard_map.95 = (bf16[2,1024,512]{2,1,0:T(8,128)(2,1)}, f32[512,1152]{1,0:T(8,128)}, f32[4608]{0:T(1024)}) custom-call(bf16[2,1024,512]{2,1,0:T(8,128)(2,1)S(1)} %get-tuple-element.6.attn, f32[512,1152]{1,0:T(8,128)S(1)} %get-tuple-element.7.total, f32[4608]{0:T(1024)S(1)} %get-tuple-element.8.gain), custom_call_target="tpu_custom_call" | custom-call | tf_op jit(solution)/shard_map/pallas_call | solution.py:500

commit v2 on v1

--- a/solution.py
+++ b/solution.py
@@ -18,7 +18,11 @@
     return index + step * (1 - 2 * (lax.div(index, step) % 2))
 
 
-HOP = 3
+HOP = 2
+EXTRA = 4
+QUEUE = 4
+OWN_LAG = 2
+EAGER = 6
 LEAD = 3
 GAP = 4
 
@@ -29,16 +33,17 @@
     proj_hbm, grad_hbm, att_hbm, w_hbm, main_hbm, gains_ref, main_gains_ref,
     attn_out, out_sum, gain_out,
     own_in, held, w_buf, att_in, att_t, acc, part, arrived,
-    gains_row, scale, shift, gain_mine, gain_got,
+    gains_row, scale, shift, gain_mine, gain_got, gain_all,
     in_sem, w_sem, att_sem, main_sem,
-    ag_send, ag_recv, pair_send, pair_recv, rs_send, rs_recv, gain_send, gain_recv,
+    ag_send, ag_recv, pair_send, pair_recv, rs_send, rs_recv, gain_send, gain_recv, share_send, share_recv,
 ):
     T, DP, D_true, micro, own, heads, wide, K, slots, ring, P, W = dims
     w = LANES
     R = micro * own
     L = (T // 2).bit_length() - 1
     C = T // 2
-    O = DP - 1
+    O = min(OWN_LAG, DP - 1)
+    A = max(O, DP - 2)
     t_me = lax.axis_index("tensor")
     d_me = lax.axis_index("dp")
     c_me, chip_me = t_me % 2, lax.div(t_me, 2)
@@ -47,7 +52,7 @@
     chip_steps = [2 << bit for bit in range(L)]
     height = R // P
     span = C * R
-    end = (K + O) * DP
+    end = (K + A) * DP
 
     blocks = 8
     group = R // blocks
@@ -85,18 +90,10 @@
 
     barrier = pltpu.get_barrier_semaphore()
     partners = [("tensor", t_pair)] + [("tensor", flip(t_me, step)) for step in chip_steps]
-    dp_steps = [1 << bit for bit in range(DP.bit_length() - 1)]
-    partners += [("dp", flip(d_me, step)) for step in dp_steps]
+    others = [lax.rem(d_me + step, DP) for step in range(1, DP)]
+    partners += [("dp", other) for other in others]
     for name, where in partners:
         pl.semaphore_signal(barrier, inc=1, device_id={name: where}, device_id_type=MESH)
-
-    @pl.when(d_me > 0)
-    def _():
-        pl.semaphore_signal(barrier, inc=1, device_id={"dp": d_me - 1}, device_id_type=MESH)
-
-    @pl.when(d_me < DP - 1)
-    def _():
-        pl.semaphore_signal(barrier, inc=1, device_id={"dp": d_me + 1}, device_id_type=MESH)
 
     def place(n):
         s, j = lax.div(n, DP), lax.rem(n, DP)
@@ -213,29 +210,38 @@
             w_load(k, d).start()
         return carry
 
-    def rs_copy(k, d, to_left):
+    def rs_copy(k, d, to_left, count):
         if to_left:
             slot = jnp.where(d_me - 1 == d, DP, d)
             peer = d_me - 1
         else:
             slot, peer = d, d_me + 1
         return pltpu.make_async_remote_copy(
-            src_ref=arrived.at[k, d], dst_ref=arrived.at[k, slot], send_sem=rs_send,
+            src_ref=arrived.at[k, d], dst_ref=arrived.at[k, slot], send_sem=rs_send.at[int(to_left), count % QUEUE],
             recv_sem=rs_recv.at[k, slot], device_id={"dp": peer}, device_id_type=MESH)
 
     def rs_arrival(k, slot):
         return pltpu.make_async_remote_copy(
-            src_ref=arrived.at[k, slot], dst_ref=arrived.at[k, slot], send_sem=rs_send,
+            src_ref=arrived.at[k, slot], dst_ref=arrived.at[k, slot], send_sem=rs_send.at[0, 0],
             recv_sem=rs_recv.at[k, slot], device_id={"dp": flip(d_me, 1)}, device_id_type=MESH)
 
-    gain_steps = [("tensor", 1)] + [("tensor", s) for s in chip_steps] + [("dp", s) for s in dp_steps]
+    gain_steps = [1] + chip_steps
     S = len(gain_steps)
 
     def gain_copy(s):
-        name, step = gain_steps[s]
         return pltpu.make_async_remote_copy(
             src_ref=gain_mine.at[s], dst_ref=gain_got.at[s], send_sem=gain_send.at[s], recv_sem=gain_recv.at[s],
-            device_id={name: flip(t_me if name == "tensor" else d_me, step)}, device_id_type=MESH)
+            device_id={"tensor": flip(t_me, gain_steps[s])}, device_id_type=MESH)
+
+    def gain_share(step):
+        return pltpu.make_async_remote_copy(
+            src_ref=gain_mine.at[S], dst_ref=gain_all.at[d_me], send_sem=share_send.at[step],
+            recv_sem=share_recv.at[d_me], device_id={"dp": others[step]}, device_id_type=MESH)
+
+    def gain_shared(step):
+        return pltpu.make_async_remote_copy(
+            src_ref=gain_mine.at[S], dst_ref=gain_all.at[others[step]], send_sem=share_send.at[step],
+            recv_sem=share_recv.at[others[step]], device_id={"dp": others[step]}, device_id_type=MESH)
 
     look = [LEAD + GAP * (L - 1 - s) for s in range(L)]
     ahead = [jnp.int32(0)] * L
@@ -256,8 +262,7 @@
         return carry
 
     finish(ahead[0])
-    waits = len(partners) + jnp.where(d_me > 0, 1, 0) + jnp.where(d_me < DP - 1, 1, 0)
-    pl.semaphore_wait(barrier, waits)
+    pl.semaphore_wait(barrier, len(partners))
     for i in range(look[0]):
         if i == look[0] - look[1] if L > 1 else i == look[0] - 1:
             lax.fori_loop(0, K, start_w, 0)
@@ -272,16 +277,22 @@
     finish(ahead[0])
     main_in.wait()
 
-    big = T * R // DP
-    gain_from = (K * DP - look[0] + 1) // 2 + DP * (DP - 1) // 2 + 1
-
-    def pass_on(n, to_left):
+    big = 2 * T * R // DP
+    pairs = DP // 2
+    gain_from = -(-(K * DP) // EAGER) + (A * DP) // 2 + 1
+
+    def pass_on(n, to_left, count):
         k, d, good = place(n)
         mine = (d < d_me) if to_left else (d > d_me)
         has_arrival = (d_me < DP - 1) if to_left else (d_me > 0)
-
-        @pl.when(jnp.logical_and(good, mine))
-        def _():
+        go = jnp.logical_and(good, mine)
+
+        @pl.when(go)
+        def _():
+            @pl.when(count >= QUEUE)
+            def _():
+                rs_copy(k, d, to_left, count).wait_send()
+
             @pl.when(has_arrival)
             def _():
                 rs_arrival(k, d).wait_recv()
@@ -291,45 +302,66 @@
             def _():
                 arrived[k, d] = part[k % ring, d].astype(jnp.bfloat16)
 
-            rs_copy(k, d, to_left).start()
-
-    def step(n, carry):
-        done, late, todo, ahead = carry[0], carry[1], carry[2], list(carry[3:])
-        k, d, good = place(n)
-        advance(n, done, L)
-        for s in reversed(range(L)):
-            advance(ahead[s], done + look[s], s, good)
-            ahead[s] = jnp.where(good, following(ahead[s]), ahead[s])
-
-        first = jnp.logical_and(good, done == 0)
-        ripe = jnp.logical_or(first, jnp.logical_and(late >= 0, jnp.logical_or(good, n - late >= 2)))
-        chosen = jnp.where(ripe, jnp.where(first, n, late), -1)
-        count = jnp.where(first, done, done - 1)
-
-        @pl.when(ripe)
-        def _():
-            k, d, _ = place(chosen)
-            pair_copy(k, d, count, 1 - c_me).wait_recv()
-            part[k % ring, d] = jnp.dot(att_t[...], held[k, d], preferred_element_type=jnp.float32)
-
-        pass_on(jnp.where(d_me == 0, chosen, n - HOP * d_me), False)
-        pass_on(jnp.where(d_me == DP - 1, chosen, n - HOP * (DP - 1 - d_me)), True)
-
-        for _ in range(2):
-            @pl.when(good)
-            def _(todo=todo):
-                finish(todo)
-            todo = jnp.where(good, following(todo), todo)
-        c = lax.div(n - 2, DP) - O - 1
-        j = lax.rem(n - 2, DP)
+            rs_copy(k, d, to_left, count).start()
+
+        return count + jnp.where(go, 1, 0)
+
+    def wait_of(hops):
+        return jnp.where(hops == 0, 2, HOP * hops + EXTRA)
+
+    def step(i, carry):
+        done, todo, rights, lefts = carry[:4]
+        ahead = list(carry[4:])
+
+        def receive(n, done, ahead):
+            good = place(n)[2]
+            advance(n, done, L)
+            moved = []
+            for s in reversed(range(L)):
+                advance(ahead[s], done + look[s], s, good)
+                moved.insert(0, jnp.where(good, following(ahead[s]), ahead[s]))
+            return done + jnp.where(good, 1, 0), moved
+
+        before = done
+        done, ahead = receive(2 * i, done, ahead)
+
+        kx, dx, gx = place(2 * i - 2)
+        ky, dy, gy = place(2 * i - 1)
+        count = before - jnp.where(gx, 1, 0) - jnp.where(gy, 1, 0)
+
+        @pl.when(jnp.logical_or(gx, gy))
+        def _():
+            tiles = ((kx, dx, gx, count), (ky, dy, gy, before - 1))
+            for k, d, g, c in tiles:
+                @pl.when(g)
+                def _(k=k, d=d, c=c):
+                    pair_copy(k, d, c, 1 - c_me).wait_recv()
+            rhs = jnp.concatenate([
+                held[jnp.where(gx, kx, ky), jnp.where(gx, dx, dy)],
+                held[jnp.where(gy, ky, kx), jnp.where(gy, dy, dx)]], axis=-1)
+            value = jnp.dot(att_t[...], rhs, preferred_element_type=jnp.float32)
+            for e, (k, d, g, c) in enumerate(tiles):
+                piece = value[:, e * w:(e + 1) * w]
+
+                @pl.when(jnp.logical_and(g, d == d_me))
+                def _(k=k, piece=piece):
+                    at = pl.ds(pl.multiple_of(k * w, w), w)
+                    out_sum[:, at] += factor * piece
+
+                @pl.when(jnp.logical_and(g, d != d_me))
+                def _(k=k, d=d, piece=piece):
+                    part[k % ring, d] = piece
+
+        done, ahead = receive(2 * i + 1, done, ahead)
+
+        c = lax.div(i, pairs) - A - 1
+        j = lax.rem(i, pairs)
 
         @pl.when(jnp.logical_and(c >= 0, c < K))
         def _():
-            @pl.when(j == 0)
-            def _():
-                @pl.when(c == 0)
-                def _():
-                    pltpu.make_async_copy(w_buf, w_buf, w_sem).wait()
+            @pl.when(jnp.logical_and(c == 0, j == 0))
+            def _():
+                pltpu.make_async_copy(w_buf, w_buf, w_sem).wait()
             rows = pl.ds(pl.multiple_of(j * big, big), big)
             lhs = jnp.concatenate([held[c, e, rows, :] for e in range(DP)], axis=-1)
             value = lax.dot_general(
@@ -347,8 +379,8 @@
             def _():
                 last = (acc[rows, :] + value).astype(jnp.bfloat16)
                 units, each = C * height // LANES, height // LANES
-                for i in range(big // LANES):
-                    at = j * (big // LANES) + i
+                for e in range(big // LANES):
+                    at = j * (big // LANES) + e
                     parity, rest = lax.div(at, P * units), lax.rem(at, P * units)
                     p, rest = lax.div(rest, units), lax.rem(rest, units)
                     index, extra = lax.div(rest, each), lax.rem(rest, each)
@@ -358,26 +390,36 @@
                     row = p * height + extra * LANES
                     m, row = lax.div(row, own), lax.rem(row, own)
                     place_in = pl.ds(pl.multiple_of((chip * 2 + parity) * own + row, LANES), LANES)
-                    attn_out[m, place_in, :] = last[i * LANES:(i + 1) * LANES]
-
-        @pl.when(jnp.logical_and(jnp.logical_and(c >= 0, c < K), j == DP - 1))
-        def _():
-            at = pl.ds(pl.multiple_of(c * w, w), w)
-            total = part[c % ring, d_me]
-            out_sum[:, at] += factor * total
+                    attn_out[m, place_in, :] = last[e * LANES:(e + 1) * LANES]
+
+        for e in range(2):
+            rights = pass_on(2 * i + e - wait_of(d_me), False, rights)
+            lefts = pass_on(2 * i + e - wait_of(DP - 1 - d_me), True, lefts)
+
+        def more(x, todo):
+            finish(todo)
+            return following(todo)
+
+        todo = lax.fori_loop(0, jnp.where(todo < end, EAGER, 0), more, todo)
+
+        f = lax.div(i, pairs) - DP
+
+        @pl.when(jnp.logical_and(jnp.logical_and(f >= 0, f < K), j == pairs - 1))
+        def _():
+            at = pl.ds(pl.multiple_of(f * w, w), w)
 
             @pl.when(d_me > 0)
             def _():
-                rs_arrival(c, d_me).wait_recv()
-                out_sum[:, at] += factor * arrived[c, d_me].astype(jnp.float32)
+                rs_arrival(f, d_me).wait_recv()
+                out_sum[:, at] += factor * arrived[f, d_me].astype(jnp.float32)
 
             @pl.when(d_me < DP - 1)
             def _():
-                rs_arrival(c, DP).wait_recv()
-                out_sum[:, at] += factor * arrived[c, DP].astype(jnp.float32)
+                rs_arrival(f, DP).wait_recv()
+                out_sum[:, at] += factor * arrived[f, DP].astype(jnp.float32)
 
         for s in range(S + 1):
-            @pl.when(n == gain_from + 2 * s)
+            @pl.when(i == gain_from + s)
             def _(s=s):
                 if s > 0:
                     gain_copy(s - 1).wait()
@@ -385,23 +427,38 @@
                 if s < S:
                     gain_copy(s).start()
                 else:
-                    gain_out[...] = main_gains_ref[...] + factor * gain_mine[s].reshape(wide)
-
-        late = jnp.where(
-            jnp.logical_and(good, jnp.logical_not(first)), n, jnp.where(ripe, -1, late))
-        return (done + jnp.where(good, 1, 0), late, todo, *ahead)
-
-    total = max(end + DP + 2, gain_from + 2 * S + 1)
-    lax.fori_loop(0, total, step, (jnp.int32(0), jnp.int32(-1), following(ahead[0]), *ahead))
+                    gain_all[d_me] = gain_mine[s]
+                    for x in range(DP - 1):
+                        gain_share(x).start()
+
+        return (done, todo, rights, lefts, *ahead)
+
+    total = max((K + A + 1) * pairs, (K + DP) * pairs, gain_from + S + 1)
+    zero = jnp.int32(0)
+    lax.fori_loop(0, total, step, (zero, following(ahead[0]), zero, zero, *ahead))
 
     def sent_all(ref, sem):
         pltpu.make_async_remote_copy(
             src_ref=ref, dst_ref=ref, send_sem=sem, recv_sem=sem,
             device_id={"tensor": t_pair}, device_id_type=MESH).wait_send()
 
+    for x in range(DP - 1):
+        gain_share(x).wait_send()
+        gain_shared(x).wait_recv()
+    gain_sum = gain_all[0]
+    for x in range(1, DP):
+        gain_sum = gain_sum + gain_all[x]
+    gain_out[...] = main_gains_ref[...] + factor * gain_sum.reshape(wide)
     sent_all(held.at[:, :, pl.ds(0, (C - 1) * R)], ag_send)
     sent_all(held.at[:, :, pl.ds(0, span)], pair_send)
-    sent_all(arrived.at[:, pl.ds(0, DP - 1)], rs_send)
+    for x in range(QUEUE):
+        @pl.when(d_me < DP - 1)
+        def _(x=x):
+            sent_all(arrived.at[0, 0], rs_send.at[0, x])
+
+        @pl.when(d_me > 0)
+        def _(x=x):
+            sent_all(arrived.at[0, 0], rs_send.at[1, x])
 
 
 def emit(attn, total, gain, attn_hbm, total_hbm, gain_hbm, sem):
@@ -455,9 +512,9 @@
     K = wide // DP // LANES
     C = T // 2
     L = C.bit_length() - 1
-    S = 1 + L + DP.bit_length() - 1
-    slots = 4
-    ring = HOP * (DP - 1) // DP + 1
+    S = 1 + L
+    slots = 2
+    ring = -(-(HOP * (DP - 2) + EXTRA) // DP)
     P = min(L, R // LANES)
     P = P if R // LANES % P == 0 else 1
     W = 1 << (LEAD + GAP * (L - 1)).bit_length()
@@ -490,8 +547,9 @@
             pltpu.VMEM((R, LANES), jnp.float32),
             pltpu.VMEM((S + 1, 1, wide), jnp.float32),
             pltpu.VMEM((S, 1, wide), jnp.float32),
+            pltpu.VMEM((DP, 1, wide), jnp.float32),
             DMA((8, 2)), DMA, DMA((slots, micro)), DMA,
-            DMA, DMA((W, L, P)), DMA, DMA((W,)), DMA, DMA((K, DP + 1)), DMA((S,)), DMA((S,)),
+            DMA, DMA((W, L, P)), DMA, DMA((W,)), DMA((2, QUEUE)), DMA((K, DP + 1)), DMA((S,)), DMA((S,)), DMA((DP - 1,)), DMA((DP,)),
         ],
         compiler_params=pltpu.CompilerParams(
             collective_id=0, has_side_effects=True, vmem_limit_bytes=VMEM_BYTES - kept

time: 110 us -> 105 us (0.955)
  Pallas kernels: 108 us -> 104 us
    pallas_call x1, Pallas kernels: 106 us -> 102 us  [per_device(): pl.pallas_call(functools.partial(kernel, dims, factor), out_shape=tuple((...]
where the time goes in v2:
time: 105 us; the launch traced here: 104 us
  Pallas kernels  104 us (99%)
    pallas_call x1, Pallas kernels, per_device(): pl.pallas_call(functools.partial(kernel, dims, factor), out_shape=tuple((...  102 us
    pallas_call x1, Pallas kernels, per_device(): pl.pallas_call(emit, out_shape=tuple((jax.ShapeDtypeStruct(shape, dtype)...  2.13 us

profile of v2, /device:TPU:0, one launch (start us, length us, event | category | flops | bytes accessed | tf_op | source)
XLA Modules:
  0.0 104.3 jit_solution(12664836974982596782)
XLA Ops:
  0.6 101.6 %shard_map.94 = (bf16[2,1024,512]{2,1,0:T(8,128)(2,1)S(1)}, f32[512,1152]{1,0:T(8,128)S(1)}, f32[4608]{0:T(1024)S(1)}) custom-call(bf16[256,4608]{1,0:T(8,128)(2,1)} %bitcast.2, bf16[256,4608]{1,0:T(8,128)(2,1)} %bitcast.3, bf16[2,1024,512]{2,1,0:T(8,128)(2,1)} %att_hbm.1, bf16[512,4608]{1,0:T(8,128)(2,1)} %w_hbm.1, f32[512,1152]{1,0:T(8,128)} %main_hbm.1, ...), custom_call_target="tpu_custom_call" | custom-call | tf_op jit(solution)/shard_map/pallas_call | solution.py:531
  102.2 2.1 %shard_map.95 = (bf16[2,1024,512]{2,1,0:T(8,128)(2,1)}, f32[512,1152]{1,0:T(8,128)}, f32[4608]{0:T(1024)}) custom-call(bf16[2,1024,512]{2,1,0:T(8,128)(2,1)S(1)} %get-tuple-element.6.attn, f32[512,1152]{1,0:T(8,128)S(1)} %get-tuple-element.7.total, f32[4608]{0:T(1024)S(1)} %get-tuple-element.8.gain), custom_call_target="tpu_custom_call" | custom-call | tf_op jit(solution)/shard_map/pallas_call | solution.py:558

commit v3 on v2

--- a/solution.py
+++ b/solution.py
@@ -19,7 +19,7 @@
 
 
 HOP = 2
-EXTRA = 4
+EXTRA = 3
 QUEUE = 4
 OWN_LAG = 2
 EAGER = 6
@@ -191,10 +191,10 @@
             src_ref=ref, dst_ref=ref, send_sem=pair_send, recv_sem=pair_recv.at[c % W],
             device_id={"tensor": t_pair}, device_id_type=MESH)
 
-    def advance(n, c, s, when=True):
+    def advance(n, c, s):
         k, d, good = place(n)
 
-        @pl.when(jnp.logical_and(good, when))
+        @pl.when(good)
         def _():
             if s > 0:
                 for copy in stage_copies(k, d, c, s - 1, True):
@@ -267,13 +267,14 @@
         if i == look[0] - look[1] if L > 1 else i == look[0] - 1:
             lax.fori_loop(0, K, start_w, 0)
             main_in.start()
-            lax.fori_loop(0, T, turn, 0)
+            lax.fori_loop(0, T // 2, turn, 0)
         for s in reversed(range(L)):
             if i - look[0] + look[s] >= 0:
                 if s == 0 and i > 0:
                     finish(ahead[0])
                 advance(ahead[s], i - look[0] + look[s], s)
                 ahead[s] = following(ahead[s])
+    lax.fori_loop(T // 2, T, turn, 0)
     finish(ahead[0])
     main_in.wait()
 
@@ -311,16 +312,22 @@
 
     def step(i, carry):
         done, todo, rights, lefts = carry[:4]
-        ahead = list(carry[4:])
+        ahead = carry[4:]
 
         def receive(n, done, ahead):
             good = place(n)[2]
             advance(n, done, L)
-            moved = []
-            for s in reversed(range(L)):
-                advance(ahead[s], done + look[s], s, good)
-                moved.insert(0, jnp.where(good, following(ahead[s]), ahead[s]))
-            return done + jnp.where(good, 1, 0), moved
+            times = jnp.where(good, 1, 0)
+
+            def issue(x, ahead):
+                moved = []
+                for s in reversed(range(L)):
+                    spot, index = ahead[2 * s], ahead[2 * s + 1]
+                    advance(spot, index, s)
+                    moved = [following(spot), index + 1] + moved
+                return tuple(moved)
+
+            return done + times, lax.fori_loop(0, times, issue, tuple(ahead))
 
         before = done
         done, ahead = receive(2 * i, done, ahead)
@@ -351,6 +358,10 @@
                 @pl.when(jnp.logical_and(g, d != d_me))
                 def _(k=k, d=d, piece=piece):
                     part[k % ring, d] = piece
+
+        for e in range(2):
+            rights = pass_on(2 * i + e - wait_of(d_me), False, rights)
+            lefts = pass_on(2 * i + e - wait_of(DP - 1 - d_me), True, lefts)
 
         done, ahead = receive(2 * i + 1, done, ahead)
 
@@ -392,10 +403,6 @@
                     place_in = pl.ds(pl.multiple_of((chip * 2 + parity) * own + row, LANES), LANES)
                     attn_out[m, place_in, :] = last[e * LANES:(e + 1) * LANES]
 
-        for e in range(2):
-            rights = pass_on(2 * i + e - wait_of(d_me), False, rights)
-            lefts = pass_on(2 * i + e - wait_of(DP - 1 - d_me), True, lefts)
-
         def more(x, todo):
             finish(todo)
             return following(todo)
@@ -435,7 +442,8 @@
 
     total = max((K + A + 1) * pairs, (K + DP) * pairs, gain_from + S + 1)
     zero = jnp.int32(0)
-    lax.fori_loop(0, total, step, (zero, following(ahead[0]), zero, zero, *ahead))
+    queue = [value for s in range(L) for value in (ahead[s], zero + look[s])]
+    lax.fori_loop(0, total, step, (zero, following(ahead[0]), zero, zero, *queue))
 
     def sent_all(ref, sem):
         pltpu.make_async_remote_copy(
@@ -513,11 +521,11 @@
     C = T // 2
     L = C.bit_length() - 1
     S = 1 + L
-    slots = 2
+    slots = 4
     ring = -(-(HOP * (DP - 2) + EXTRA) // DP)
     P = min(L, R // LANES)
     P = P if R // LANES % P == 0 else 1
-    W = 1 << (LEAD + GAP * (L - 1)).bit_length()
+    W = LEAD + GAP * (L - 1) + 1
     dims = (T, DP, D, micro, own, heads, wide, K, slots, ring, P, W)
     DMA = pltpu.SemaphoreType.DMA
     hbm = pl.BlockSpec(memory_space=pltpu.HBM)

time: 105 us -> 99.9 us (0.951)
  Pallas kernels: 104 us -> 98.1 us
    pallas_call x1, Pallas kernels: 102 us -> 96 us  [per_device(): pl.pallas_call(functools.partial(kernel, dims, factor), out_shape=tuple((...]
where the time goes in v3:
time: 99.9 us; the launch traced here: 98.8 us
  Pallas kernels  98.1 us (98%)
    pallas_call x1, Pallas kernels, per_device(): pl.pallas_call(functools.partial(kernel, dims, factor), out_shape=tuple((...  96 us
    pallas_call x1, Pallas kernels, per_device(): pl.pallas_call(emit, out_shape=tuple((jax.ShapeDtypeStruct(shape, dtype)...  2.13 us

profile of v3, /device:TPU:0, one launch (start us, length us, event | category | flops | bytes accessed | tf_op | source)
XLA Modules:
  0.0 98.8 jit_solution(17971870232917737473)
XLA Ops:
  0.6 96.0 %shard_map.94 = (bf16[2,1024,512]{2,1,0:T(8,128)(2,1)S(1)}, f32[512,1152]{1,0:T(8,128)S(1)}, f32[4608]{0:T(1024)S(1)}) custom-call(bf16[256,4608]{1,0:T(8,128)(2,1)} %bitcast.2, bf16[256,4608]{1,0:T(8,128)(2,1)} %bitcast.3, bf16[2,1024,512]{2,1,0:T(8,128)(2,1)} %att_hbm.1, bf16[512,4608]{1,0:T(8,128)(2,1)} %w_hbm.1, f32[512,1152]{1,0:T(8,128)} %main_hbm.1, ...), custom_call_target="tpu_custom_call" | custom-call | tf_op jit(solution)/shard_map/pallas_call | solution.py:539
  96.6 2.1 %shard_map.95 = (bf16[2,1024,512]{2,1,0:T(8,128)(2,1)}, f32[512,1152]{1,0:T(8,128)}, f32[4608]{0:T(1024)}) custom-call(bf16[2,1024,512]{2,1,0:T(8,128)(2,1)S(1)} %get-tuple-element.6.attn, f32[512,1152]{1,0:T(8,128)S(1)} %get-tuple-element.7.total, f32[4608]{0:T(1024)S(1)} %get-tuple-element.8.gain), custom_call_target="tpu_custom_call" | custom-call | tf_op jit(solution)/shard_map/pallas_call | solution.py:566
